TPU v7x, 32 devices: a whole 2x2x4 slice. The times are simulated.
32 devices in a mesh: ta: 2 (over x), gz: 4 (over z), xy: 4 (over y, core).
Axes of the slice: x: 2, y: 2, z: 4, core: 2. Of those that a mesh axis runs over, the one named last changes fastest.
Arguments:
- source: float32 [2, 48, 2, 4, 512], P(None, None, 'ta', 'gz', 'xy'), may hold values from -14 to 14
- inverse: bfloat16 [2, 48, 48, 2, 4, 512], P(None, None, None, 'ta', 'gz', 'xy'), may hold values from -0.625 to 0.625
- coarse_links: bfloat16 [8, 2, 48, 48, 2, 4, 512], P(None, None, None, None, 'ta', 'gz', 'xy'), may hold values from -0.15625 to 0.15625
Outputs:
- solution: float32 [2, 48, 2, 4, 512], P(None, None, 'ta', 'gz', 'xy')
- residual: float32 [2, 48, 2, 4, 512], P(None, None, 'ta', 'gz', 'xy')
- hessenberg: float32 [2, 6, 5], replicated
All inputs are finite; a program needn't handle non-finite values.
Results may differ from a plain program's by a relative error of at most 0.0003.
Values sent between devices are 32-bit elements; how exact they have to be, the bound alone decides.
A program may use at most 128 MiB of HBM per device.

v0:
```python
import jax
import jax.numpy as jnp
from jax import lax
from jax.sharding import PartitionSpec as P

LY = 16
ITERS = 5


def padded_2(cells, sides, width):
    for axis, dim in sides:
        count = lax.axis_size(axis)
        head = lax.slice_in_dim(cells, 0, width, axis=dim)
        tail = lax.slice_in_dim(cells, cells.shape[dim] - width, cells.shape[dim], axis=dim)
        cells = jnp.concatenate(
            [
                lax.ppermute(tail, axis, [(i, (i + 1) % count) for i in range(count)]),
                cells,
                lax.ppermute(head, axis, [((i + 1) % count, i) for i in range(count)]),
            ],
            axis=dim,
        )
    return cells


def block_apply(blocks, vector):
    real_blocks = blocks[0].astype(jnp.float32)
    imag_blocks = blocks[1].astype(jnp.float32)
    vec_real = vector[0][None]
    vec_imag = vector[1][None]
    real_part = jnp.sum(real_blocks * vec_real - imag_blocks * vec_imag, axis=1)
    imag_part = jnp.sum(real_blocks * vec_imag + imag_blocks * vec_real, axis=1)
    return jnp.stack([real_part, imag_part])


def complex_dot(left, right):
    real_part = jnp.sum(left[0] * right[0] + left[1] * right[1])
    imag_part = jnp.sum(left[0] * right[1] - left[1] * right[0])
    return (real_part, imag_part)


def scaled(coef_real, coef_imag, vector):
    return jnp.stack(
        [
            coef_real * vector[0] - coef_imag * vector[1],
            coef_real * vector[1] + coef_imag * vector[0],
        ]
    )


def y_neighbours(field):
    positions = jnp.arange(field.shape[4]) % LY
    is_last = positions == LY - 1
    is_first = positions == 0
    forward = jnp.where(is_last, jnp.roll(field, LY - 1, axis=4), jnp.roll(field, -1, axis=4))
    backward = jnp.where(is_first, jnp.roll(field, 1 - LY, axis=4), jnp.roll(field, 1, axis=4))
    return (forward, backward)


def apply_operator(field, inverse, coarse_links):
    padded = padded_2(field, (("ta", 2), ("gz", 3)), 1)
    widened = padded_2(field, (("xy", 4),), LY)
    extent = field.shape[4]
    forward_y, backward_y = y_neighbours(field)
    neighbours = [
        padded[:, :, 2:, 1:-1],
        padded[:, :, :-2, 1:-1],
        padded[:, :, 1:-1, 2:],
        padded[:, :, 1:-1, :-2],
        widened[..., 2 * LY : 2 * LY + extent],
        widened[..., :extent],
        forward_y,
        backward_y,
    ]
    hopping = block_apply(coarse_links[0], neighbours[0])
    for d in range(1, 8):
        hopping = hopping + block_apply(coarse_links[d], neighbours[d])
    return field + block_apply(inverse, hopping)


def solve_small(hessenberg, source_norm):
    upper_half = jnp.concatenate([hessenberg[0], -hessenberg[1]], axis=1)
    lower_half = jnp.concatenate([hessenberg[1], hessenberg[0]], axis=1)
    real_form = jnp.concatenate([upper_half, lower_half], axis=0)
    target = jnp.zeros((2 * (ITERS + 1),), jnp.float32).at[0].set(source_norm)
    normal_mat = jnp.dot(real_form.T, real_form, precision=lax.Precision.HIGHEST)
    projected = jnp.dot(real_form.T, target, precision=lax.Precision.HIGHEST)
    factor = jnp.linalg.cholesky(normal_mat)
    forward_vals = []
    for i in range(2 * ITERS):
        partial_sum = projected[i]
        for k in range(i):
            partial_sum = partial_sum - factor[i, k] * forward_vals[k]
        forward_vals.append(partial_sum / factor[i, i])
    solved = [None] * (2 * ITERS)
    for i in reversed(range(2 * ITERS)):
        partial_sum = forward_vals[i]
        for k in range(i + 1, 2 * ITERS):
            partial_sum = partial_sum - factor[k, i] * solved[k]
        solved[i] = partial_sum / factor[i, i]
    coeffs = jnp.stack(solved)
    return (coeffs[:ITERS], coeffs[ITERS:], target)


def per_device(source, inverse, coarse_links):
    norm_sq = lax.psum(complex_dot(source, source)[0], ("ta", "gz", "xy"))
    source_norm = jnp.sqrt(norm_sq)
    krylov_basis = [source / source_norm]
    hessenberg = jnp.zeros((2, ITERS + 1, ITERS), jnp.float32)
    for j in range(ITERS):
        candidate = apply_operator(krylov_basis[j], inverse, coarse_links)
        local_pairs = [complex_dot(krylov_basis[i], candidate) for i in range(j + 1)]
        whole_local = complex_dot(candidate, candidate)[0]
        proj_reals, proj_imags, whole_sq = lax.psum(
            (
                jnp.stack([entry[0] for entry in local_pairs]),
                jnp.stack([entry[1] for entry in local_pairs]),
                whole_local,
            ),
            ("ta", "gz", "xy"),
        )
        for i in range(j + 1):
            candidate = candidate - scaled(proj_reals[i], proj_imags[i], krylov_basis[i])
            hessenberg = hessenberg.at[0, i, j].set(proj_reals[i]).at[1, i, j].set(proj_imags[i])
        length_sq = whole_sq - jnp.sum(proj_reals * proj_reals + proj_imags * proj_imags)
        length = jnp.sqrt(length_sq)
        hessenberg = hessenberg.at[0, j + 1, j].set(length)
        krylov_basis.append(candidate / length)
    coef_real, coef_imag, target = solve_small(hessenberg, source_norm)
    solution = scaled(coef_real[0], coef_imag[0], krylov_basis[0])
    for j in range(1, ITERS):
        solution = solution + scaled(coef_real[j], coef_imag[j], krylov_basis[j])
    residual = source - apply_operator(solution, inverse, coarse_links)
    return (solution, residual, hessenberg)


def solution(mesh):
    return jax.shard_map(
        per_device,
        mesh=mesh,
        in_specs=(
            P(None, None, "ta", "gz", "xy"),
            P(None, None, None, "ta", "gz", "xy"),
            P(None, None, None, None, "ta", "gz", "xy"),
        ),
        out_specs=(P(None, None, "ta", "gz", "xy"), P(None, None, "ta", "gz", "xy"), P()),
        check_vma=False,
    )
```

profile of v0, /device:TPU:0, one launch (start us, length us, event | category | flops | bytes accessed | tf_op | source)
XLA Modules:
  0.0 561.9 jit_solution(17427624493626627391)
XLA Ops:
  2.1 42.2 %psum.112 = f32[]{:T(128)} all-reduce(f32[]{:T(128)} %add_reduce_fusion.20), channel_id=1, replica_groups=mesh['ta'=2,'gz'=4,'xy'=4] {'ta','gz','xy'}, use_global_device_ids=true, to_apply=%region_1.0 | all-reduce | flops 1 | bytes 8 | tf_op jit(solution)/shard_map/psum | solution.py:106
  53.1 3.7 fusion.169
  59.2 3.0 fusion.25
  63.5 4.9 collective-permute-done.3
  68.4 3.8 fusion.97
  73.8 38.8 %all-reduce.6 = (f32[1]{0:T(128)}, f32[1]{0:T(128)}, f32[]{:T(128)}) all-reduce(f32[1]{0:T(128)} %bitcast.81, f32[1]{0:T(128)} %bitcast.83, f32[]{:T(128)} %get-tuple-element.653), channel_id=1, replica_groups=mesh['ta'=2,'gz'=4,'xy'=4] {'ta','gz','xy'}, use_global_device_ids=true, to_apply=%region_21.22 | all-reduce | flops 3 | bytes 24 | tf_op jit(solution)/shard_map/psum | solution.py:114
  125.7 3.7 fusion.173
  133.4 3.0 fusion.29
  139.9 3.7 fusion.101
  148.0 38.8 %all-reduce.5 = (f32[2]{0:T(128)S(1)}, f32[2]{0:T(128)S(1)}, f32[]{:T(128)}) all-reduce(f32[2]{0:T(128)S(1)} %pad_maximum_fusion.30, f32[2]{0:T(128)S(1)} %pad_maximum_fusion.31, f32[]{:T(128)} %get-tuple-element.650), channel_id=1, replica_groups=mesh['ta'=2,'gz'=4,'xy'=4] {'ta','gz','xy'}, use_global_device_ids=true, to_apply=%region_46.47 | all-reduce | flops 5 | bytes 40 | tf_op jit(solution)/shard_map/psum | solution.py:114
  201.3 3.7 fusion.177
  207.2 3.0 fusion.33
  211.1 4.2 collective-permute-done.15
  215.3 3.7 fusion.105
  224.6 39.9 %all-reduce.4 = (f32[3]{0:T(128)S(1)}, f32[3]{0:T(128)S(1)}, f32[]{:T(128)}) all-reduce(f32[3]{0:T(128)S(1)} %pad_maximum_fusion.32, f32[3]{0:T(128)S(1)} %pad_maximum_fusion.33, f32[]{:T(128)} %get-tuple-element.647), channel_id=1, replica_groups=mesh['ta'=2,'gz'=4,'xy'=4] {'ta','gz','xy'}, use_global_device_ids=true, to_apply=%region_74.75 | all-reduce | flops 7 | bytes 56 | tf_op jit(solution)/shard_map/psum | solution.py:114
  277.9 2.7 scatter.136
  283.6 3.7 fusion.181
  289.5 3.0 fusion.37
  293.4 4.6 collective-permute-done.21
  298.1 3.7 fusion.109
  308.8 39.9 %all-reduce.3 = (f32[4]{0:T(128)S(1)}, f32[4]{0:T(128)S(1)}, f32[]{:T(128)}) all-reduce(f32[4]{0:T(128)S(1)} %pad_maximum_fusion.34, f32[4]{0:T(128)S(1)} %pad_maximum_fusion.35, f32[]{:T(128)} %get-tuple-element.642), channel_id=1, replica_groups=mesh['ta'=2,'gz'=4,'xy'=4] {'ta','gz','xy'}, use_global_device_ids=true, to_apply=%region_104.105 | all-reduce | flops 9 | bytes 72 | tf_op jit(solution)/shard_map/psum | solution.py:114
  368.9 3.7 fusion.185
  374.9 3.0 fusion.41
  378.7 4.4 collective-permute-done.27
  383.2 3.7 fusion.113
  389.1 3.2 stack.868
  392.3 3.3 stack.862
  395.6 40.1 %all-reduce.2 = (f32[5]{0:T(128)S(1)}, f32[5]{0:T(128)S(1)}, f32[]{:T(128)}) all-reduce(f32[5]{0:T(128)S(1)} %stack.862, f32[5]{0:T(128)S(1)} %stack.868, f32[]{:T(128)} %get-tuple-element.751), channel_id=1, replica_groups=mesh['ta'=2,'gz'=4,'xy'=4] {'ta','gz','xy'}, use_global_device_ids=true, to_apply=%region_136.137 | all-reduce | flops 11 | bytes 88 | tf_op jit(solution)/shard_map/psum | solution.py:114
  542.8 3.7 fusion.189
  548.8 3.0 fusion.45
  552.8 3.5 collective-permute-done.33
  556.3 3.7 fusion.117
  (290 shorter events, 140.4 us)
Async XLA Ops:
  45.8 11.1 %collective-permute-start = (f32[2,48,1,1,128]{4,3,2,1,0:T(1,128)S(1)}, f32[2,48,1,1,128]{4,3,2,1,0:T(1,128)S(1)}, u32[]{:S(2)}, u32[]{:S(2)}) collective-permute-start(f32[2,48,1,1,128]{4,3,2,1,0:T(1,128)S(1)} %broadcast_divide_fusion), channel_id=1, source_target_pairs={{16,0},{0,16},{17,1},{1,17},{18,2},{2,18},{19,3},{3,19},{20,4},{4,... | collective-permute-start | bytes 147464 | tf_op jit(solution)/shard_map/ppermute | solution.py:19
  48.1 8.7 %collective-permute-start.1 = (f32[2,48,1,1,128]{4,3,2,1,0:T(1,128)S(1)}, f32[2,48,1,1,128]{4,3,2,1,0:T(1,128)S(1)}, u32[]{:S(2)}, u32[]{:S(2)}) collective-permute-start(f32[2,48,1,1,128]{4,3,2,1,0:T(1,128)S(1)} %broadcast_divide_fusion), channel_id=1, source_target_pairs={{0,16},{16,0},{1,17},{17,1},{2,18},{18,2},{3,19},{19,3},{4,20},{20... | collective-permute-start | bytes 147464 | tf_op jit(solution)/shard_map/ppermute | solution.py:17
  48.4 4.4 collective-permute-start.5
  57.0 6.5 %collective-permute-start.2 = (f32[2,48,3,1,128]{4,3,2,1,0:T(1,128)S(1)}, f32[2,48,3,1,128]{4,3,2,1,0:T(1,128)S(1)}, u32[]{:S(2)}, u32[]{:S(2)}) collective-permute-start(f32[2,48,3,1,128]{4,3,2,1,0:T(1,128)S(1)} %pad_maximum_fusion), channel_id=1, source_target_pairs={{4,0},{8,4},{12,8},{0,12},{5,1},{9,5},{13,9},{1,13},{6,2},{10,6},{... | collective-permute-start | bytes 442376 | tf_op jit(solution)/shard_map/ppermute | solution.py:19
  59.2 9.1 %collective-permute-start.3 = (f32[2,48,3,1,128]{4,3,2,1,0:T(1,128)S(1)}, f32[2,48,3,1,128]{4,3,2,1,0:T(1,128)S(1)}, u32[]{:S(2)}, u32[]{:S(2)}) collective-permute-start(f32[2,48,3,1,128]{4,3,2,1,0:T(1,128)S(1)} %pad_maximum_fusion), channel_id=1, source_target_pairs={{0,4},{4,8},{8,12},{12,0},{1,5},{5,9},{9,13},{13,1},{2,6},{6,10},{... | collective-permute-start | bytes 442376 | tf_op jit(solution)/shard_map/ppermute | solution.py:17
  118.2 11.2 %collective-permute-start.6 = (f32[2,48,1,1,128]{4,3,2,1,0:T(1,128)S(1)}, f32[2,48,1,1,128]{4,3,2,1,0:T(1,128)S(1)}, u32[]{:S(2)}, u32[]{:S(2)}) collective-permute-start(f32[2,48,1,1,128]{4,3,2,1,0:T(1,128)S(1)} %fusion.222), channel_id=1, source_target_pairs={{16,0},{0,16},{17,1},{1,17},{18,2},{2,18},{19,3},{3,19},{20,4},{4,... | collective-permute-start | bytes 147464 | tf_op jit(solution)/shard_map/ppermute | solution.py:19
  120.5 8.9 %collective-permute-start.7 = (f32[2,48,1,1,128]{4,3,2,1,0:T(1,128)S(1)}, f32[2,48,1,1,128]{4,3,2,1,0:T(1,128)S(1)}, u32[]{:S(2)}, u32[]{:S(2)}) collective-permute-start(f32[2,48,1,1,128]{4,3,2,1,0:T(1,128)S(1)} %fusion.222), channel_id=1, source_target_pairs={{0,16},{16,0},{1,17},{17,1},{2,18},{18,2},{3,19},{19,3},{4,20},{20... | collective-permute-start | bytes 147464 | tf_op jit(solution)/shard_map/ppermute | solution.py:17
  121.0 4.4 collective-permute-start.11
  129.6 8.6 %collective-permute-start.9 = (f32[2,48,3,1,128]{4,3,2,1,0:T(1,128)S(1)}, f32[2,48,3,1,128]{4,3,2,1,0:T(1,128)S(1)}, u32[]{:S(2)}, u32[]{:S(2)}) collective-permute-start(f32[2,48,3,1,128]{4,3,2,1,0:T(1,128)S(1)} %pad_maximum_fusion.1), channel_id=1, source_target_pairs={{0,4},{4,8},{8,12},{12,0},{1,5},{5,9},{9,13},{13,1},{2,6},{6,10},{... | collective-permute-start | bytes 442376 | tf_op jit(solution)/shard_map/ppermute | solution.py:17
  131.1 8.8 %collective-permute-start.8 = (f32[2,48,3,1,128]{4,3,2,1,0:T(1,128)S(1)}, f32[2,48,3,1,128]{4,3,2,1,0:T(1,128)S(1)}, u32[]{:S(2)}, u32[]{:S(2)}) collective-permute-start(f32[2,48,3,1,128]{4,3,2,1,0:T(1,128)S(1)} %pad_maximum_fusion.1), channel_id=1, source_target_pairs={{4,0},{8,4},{12,8},{0,12},{5,1},{9,5},{13,9},{1,13},{6,2},{10,6},{... | collective-permute-start | bytes 442376 | tf_op jit(solution)/shard_map/ppermute | solution.py:19
  193.7 11.3 %collective-permute-start.12 = (f32[2,48,1,1,128]{4,3,2,1,0:T(1,128)S(1)}, f32[2,48,1,1,128]{4,3,2,1,0:T(1,128)S(1)}, u32[]{:S(2)}, u32[]{:S(2)}) collective-permute-start(f32[2,48,1,1,128]{4,3,2,1,0:T(1,128)S(1)} %fusion.262), channel_id=1, source_target_pairs={{16,0},{0,16},{17,1},{1,17},{18,2},{2,18},{19,3},{3,19},{20,4},{4,... | collective-permute-start | bytes 147464 | tf_op jit(solution)/shard_map/ppermute | solution.py:19
  196.0 9.0 %collective-permute-start.13 = (f32[2,48,1,1,128]{4,3,2,1,0:T(1,128)S(1)}, f32[2,48,1,1,128]{4,3,2,1,0:T(1,128)S(1)}, u32[]{:S(2)}, u32[]{:S(2)}) collective-permute-start(f32[2,48,1,1,128]{4,3,2,1,0:T(1,128)S(1)} %fusion.262), channel_id=1, source_target_pairs={{0,16},{16,0},{1,17},{17,1},{2,18},{18,2},{3,19},{19,3},{4,20},{20... | collective-permute-start | bytes 147464 | tf_op jit(solution)/shard_map/ppermute | solution.py:17
  196.4 4.5 collective-permute-start.16
  196.5 4.4 collective-permute-start.17
  205.1 5.9 %collective-permute-start.14 = (f32[2,48,3,1,128]{4,3,2,1,0:T(1,128)S(1)}, f32[2,48,3,1,128]{4,3,2,1,0:T(1,128)S(1)}, u32[]{:S(2)}, u32[]{:S(2)}) collective-permute-start(f32[2,48,3,1,128]{4,3,2,1,0:T(1,128)S(1)} %pad_maximum_fusion.2), channel_id=1, source_target_pairs={{4,0},{8,4},{12,8},{0,12},{5,1},{9,5},{13,9},{1,13},{6,2},{10,6},{... | collective-permute-start | bytes 442376 | tf_op jit(solution)/shard_map/ppermute | solution.py:19
  206.8 8.5 %collective-permute-start.15 = (f32[2,48,3,1,128]{4,3,2,1,0:T(1,128)S(1)}, f32[2,48,3,1,128]{4,3,2,1,0:T(1,128)S(1)}, u32[]{:S(2)}, u32[]{:S(2)}) collective-permute-start(f32[2,48,3,1,128]{4,3,2,1,0:T(1,128)S(1)} %pad_maximum_fusion.2), channel_id=1, source_target_pairs={{0,4},{4,8},{8,12},{12,0},{1,5},{5,9},{9,13},{13,1},{2,6},{6,10},{... | collective-permute-start | bytes 442376 | tf_op jit(solution)/shard_map/ppermute | solution.py:17
  272.8 14.4 %collective-permute-start.18 = (f32[2,48,1,1,128]{4,3,2,1,0:T(1,128)S(1)}, f32[2,48,1,1,128]{4,3,2,1,0:T(1,128)S(1)}, u32[]{:S(2)}, u32[]{:S(2)}) collective-permute-start(f32[2,48,1,1,128]{4,3,2,1,0:T(1,128)S(1)} %fusion.263), channel_id=1, source_target_pairs={{16,0},{0,16},{17,1},{1,17},{18,2},{2,18},{19,3},{3,19},{20,4},{4,... | collective-permute-start | bytes 147464 | tf_op jit(solution)/shard_map/ppermute | solution.py:19
  275.2 12.1 %collective-permute-start.19 = (f32[2,48,1,1,128]{4,3,2,1,0:T(1,128)S(1)}, f32[2,48,1,1,128]{4,3,2,1,0:T(1,128)S(1)}, u32[]{:S(2)}, u32[]{:S(2)}) collective-permute-start(f32[2,48,1,1,128]{4,3,2,1,0:T(1,128)S(1)} %fusion.263), channel_id=1, source_target_pairs={{0,16},{16,0},{1,17},{17,1},{2,18},{18,2},{3,19},{19,3},{4,20},{20... | collective-permute-start | bytes 147464 | tf_op jit(solution)/shard_map/ppermute | solution.py:17
  275.5 7.7 %collective-permute-start.22 = (f32[2,48,1,1,16]{4,3,2,1,0:T(1,128)S(1)}, f32[2,48,1,1,16]{4,3,2,1,0:T(1,128)S(1)}, u32[]{:S(2)}, u32[]{:S(2)}) collective-permute-start(f32[2,48,1,1,16]{4,3,2,1,0:T(1,128)S(1)} %get-tuple-element.797), channel_id=1, source_target_pairs={{1,0},{2,1},{3,2},{0,3},{5,4},{6,5},{7,6},{4,7},{9,8},{10,9},{11,1... | collective-permute-start | bytes 18440 | tf_op jit(solution)/shard_map/ppermute | solution.py:19
  275.6 7.6 %collective-permute-start.23 = (f32[2,48,1,1,16]{4,3,2,1,0:T(1,128)S(1)}, f32[2,48,1,1,16]{4,3,2,1,0:T(1,128)S(1)}, u32[]{:S(2)}, u32[]{:S(2)}) collective-permute-start(f32[2,48,1,1,16]{4,3,2,1,0:T(1,128)S(1)} %get-tuple-element.796), channel_id=1, source_target_pairs={{0,1},{1,2},{2,3},{3,0},{4,5},{5,6},{6,7},{7,4},{8,9},{9,10},{10,1... | collective-permute-start | bytes 18440 | tf_op jit(solution)/shard_map/ppermute | solution.py:17
  287.4 5.9 %collective-permute-start.20 = (f32[2,48,3,1,128]{4,3,2,1,0:T(1,128)S(1)}, f32[2,48,3,1,128]{4,3,2,1,0:T(1,128)S(1)}, u32[]{:S(2)}, u32[]{:S(2)}) collective-permute-start(f32[2,48,3,1,128]{4,3,2,1,0:T(1,128)S(1)} %pad_maximum_fusion.3), channel_id=1, source_target_pairs={{4,0},{8,4},{12,8},{0,12},{5,1},{9,5},{13,9},{1,13},{6,2},{10,6},{... | collective-permute-start | bytes 442376 | tf_op jit(solution)/shard_map/ppermute | solution.py:19
  289.5 8.5 %collective-permute-start.21 = (f32[2,48,3,1,128]{4,3,2,1,0:T(1,128)S(1)}, f32[2,48,3,1,128]{4,3,2,1,0:T(1,128)S(1)}, u32[]{:S(2)}, u32[]{:S(2)}) collective-permute-start(f32[2,48,3,1,128]{4,3,2,1,0:T(1,128)S(1)} %pad_maximum_fusion.3), channel_id=1, source_target_pairs={{0,4},{4,8},{8,12},{12,0},{1,5},{5,9},{9,13},{13,1},{2,6},{6,10},{... | collective-permute-start | bytes 442376 | tf_op jit(solution)/shard_map/ppermute | solution.py:17
  358.5 14.2 %collective-permute-start.24 = (f32[2,48,1,1,128]{4,3,2,1,0:T(1,128)S(1)}, f32[2,48,1,1,128]{4,3,2,1,0:T(1,128)S(1)}, u32[]{:S(2)}, u32[]{:S(2)}) collective-permute-start(f32[2,48,1,1,128]{4,3,2,1,0:T(1,128)S(1)} %fusion.246), channel_id=1, source_target_pairs={{16,0},{0,16},{17,1},{1,17},{18,2},{2,18},{19,3},{3,19},{20,4},{4,... | collective-permute-start | bytes 147464 | tf_op jit(solution)/shard_map/ppermute | solution.py:19
  360.8 11.8 %collective-permute-start.25 = (f32[2,48,1,1,128]{4,3,2,1,0:T(1,128)S(1)}, f32[2,48,1,1,128]{4,3,2,1,0:T(1,128)S(1)}, u32[]{:S(2)}, u32[]{:S(2)}) collective-permute-start(f32[2,48,1,1,128]{4,3,2,1,0:T(1,128)S(1)} %fusion.246), channel_id=1, source_target_pairs={{0,16},{16,0},{1,17},{17,1},{2,18},{18,2},{3,19},{19,3},{4,20},{20... | collective-permute-start | bytes 147464 | tf_op jit(solution)/shard_map/ppermute | solution.py:17
  361.2 7.4 %collective-permute-start.28 = (f32[2,48,1,1,16]{4,3,2,1,0:T(1,128)S(1)}, f32[2,48,1,1,16]{4,3,2,1,0:T(1,128)S(1)}, u32[]{:S(2)}, u32[]{:S(2)}) collective-permute-start(f32[2,48,1,1,16]{4,3,2,1,0:T(1,128)S(1)} %get-tuple-element.763), channel_id=1, source_target_pairs={{1,0},{2,1},{3,2},{0,3},{5,4},{6,5},{7,6},{4,7},{9,8},{10,9},{11,1... | collective-permute-start | bytes 18440 | tf_op jit(solution)/shard_map/ppermute | solution.py:19
  361.2 7.3 %collective-permute-start.29 = (f32[2,48,1,1,16]{4,3,2,1,0:T(1,128)S(1)}, f32[2,48,1,1,16]{4,3,2,1,0:T(1,128)S(1)}, u32[]{:S(2)}, u32[]{:S(2)}) collective-permute-start(f32[2,48,1,1,16]{4,3,2,1,0:T(1,128)S(1)} %get-tuple-element.762), channel_id=1, source_target_pairs={{0,1},{1,2},{2,3},{3,0},{4,5},{5,6},{6,7},{7,4},{8,9},{9,10},{10,1... | collective-permute-start | bytes 18440 | tf_op jit(solution)/shard_map/ppermute | solution.py:17
  372.8 5.9 %collective-permute-start.26 = (f32[2,48,3,1,128]{4,3,2,1,0:T(1,128)S(1)}, f32[2,48,3,1,128]{4,3,2,1,0:T(1,128)S(1)}, u32[]{:S(2)}, u32[]{:S(2)}) collective-permute-start(f32[2,48,3,1,128]{4,3,2,1,0:T(1,128)S(1)} %pad_maximum_fusion.4), channel_id=1, source_target_pairs={{4,0},{8,4},{12,8},{0,12},{5,1},{9,5},{13,9},{1,13},{6,2},{10,6},{... | collective-permute-start | bytes 442376 | tf_op jit(solution)/shard_map/ppermute | solution.py:19
  374.9 8.3 %collective-permute-start.27 = (f32[2,48,3,1,128]{4,3,2,1,0:T(1,128)S(1)}, f32[2,48,3,1,128]{4,3,2,1,0:T(1,128)S(1)}, u32[]{:S(2)}, u32[]{:S(2)}) collective-permute-start(f32[2,48,3,1,128]{4,3,2,1,0:T(1,128)S(1)} %pad_maximum_fusion.4), channel_id=1, source_target_pairs={{0,4},{4,8},{8,12},{12,0},{1,5},{5,9},{9,13},{13,1},{2,6},{6,10},{... | collective-permute-start | bytes 442376 | tf_op jit(solution)/shard_map/ppermute | solution.py:17
  535.3 11.2 %collective-permute-start.30 = (f32[2,48,1,1,128]{4,3,2,1,0:T(1,128)S(1)}, f32[2,48,1,1,128]{4,3,2,1,0:T(1,128)S(1)}, u32[]{:S(2)}, u32[]{:S(2)}) collective-permute-start(f32[2,48,1,1,128]{4,3,2,1,0:T(1,128)S(1)} %maximum_add_fusion.11), channel_id=1, source_target_pairs={{16,0},{0,16},{17,1},{1,17},{18,2},{2,18},{19,3},{3,19},{20,4},{4,... | collective-permute-start | bytes 147464 | tf_op jit(solution)/shard_map/ppermute | solution.py:19
  537.7 8.8 %collective-permute-start.31 = (f32[2,48,1,1,128]{4,3,2,1,0:T(1,128)S(1)}, f32[2,48,1,1,128]{4,3,2,1,0:T(1,128)S(1)}, u32[]{:S(2)}, u32[]{:S(2)}) collective-permute-start(f32[2,48,1,1,128]{4,3,2,1,0:T(1,128)S(1)} %maximum_add_fusion.11), channel_id=1, source_target_pairs={{0,16},{16,0},{1,17},{17,1},{2,18},{18,2},{3,19},{19,3},{4,20},{20... | collective-permute-start | bytes 147464 | tf_op jit(solution)/shard_map/ppermute | solution.py:17
  546.7 6.0 %collective-permute-start.32 = (f32[2,48,3,1,128]{4,3,2,1,0:T(1,128)S(1)}, f32[2,48,3,1,128]{4,3,2,1,0:T(1,128)S(1)}, u32[]{:S(2)}, u32[]{:S(2)}) collective-permute-start(f32[2,48,3,1,128]{4,3,2,1,0:T(1,128)S(1)} %pad_maximum_fusion.5), channel_id=1, source_target_pairs={{4,0},{8,4},{12,8},{0,12},{5,1},{9,5},{13,9},{1,13},{6,2},{10,6},{... | collective-permute-start | bytes 442376 | tf_op jit(solution)/shard_map/ppermute | solution.py:19
  548.4 7.9 %collective-permute-start.33 = (f32[2,48,3,1,128]{4,3,2,1,0:T(1,128)S(1)}, f32[2,48,3,1,128]{4,3,2,1,0:T(1,128)S(1)}, u32[]{:S(2)}, u32[]{:S(2)}) collective-permute-start(f32[2,48,3,1,128]{4,3,2,1,0:T(1,128)S(1)} %pad_maximum_fusion.5), channel_id=1, source_target_pairs={{0,4},{4,8},{8,12},{12,0},{1,5},{5,9},{9,13},{13,1},{2,6},{6,10},{... | collective-permute-start | bytes 442376 | tf_op jit(solution)/shard_map/ppermute | solution.py:17
  (8 other events, 80.2 us)
where the time goes:
time: 573 us; the launch traced here: 562 us
  blocking collectives  240 us (42%)
  other arithmetic  112 us (20%)
  between operations  88.9 us (16%)
  local copies, waits for them, and re-layouts  52.9 us (9%)
  waiting for transfers between devices  35.3 us (6%)
  starting transfers between devices  32.3 us (6%)
    psum x5, blocking collectives, per_device(): lax.psum((jnp.stack([entry[0] for entry in local_pairs]), jnp.stack([entr...  198 us
    reduce_sum x24, other arithmetic, block_apply(): real_part = jnp.sum(real_blocks * vec_real - imag_blocks * vec_imag, axis=1)  65.3 us
    psum x1, blocking collectives, per_device(): norm_sq = lax.psum(complex_dot(source, source)[0], ('ta', 'gz', 'xy'))  42.2 us
    ppermute x18, waiting for transfers between devices, padded_2(): lax.ppermute(tail, axis, [(i, (i + 1) % count) for i in range(count)])  28.5 us
    ppermute x18, starting transfers between devices, padded_2(): lax.ppermute(head, axis, [((i + 1) % count, i) for i in range(count)])  26.5 us
    scatter x30, local copies, waits for them, and re-layouts, per_device(): hessenberg.at[0, i, j].set(proj_reals[i]).at[1, i, j].set(proj_imags[i])  25.8 us
    sub x15, other arithmetic, scaled(): coef_real * vector[0] - coef_imag * vector[1]  13.2 us
  transfers between devices with their start and end apart: 36, of which 16 were waited for; matrix products, arithmetic and copies ran while one was open for 12% of the time, Pallas kernels for 0%

commit v1 on v0

--- a/solution.py
+++ b/solution.py
@@ -5,6 +5,11 @@
 
 LY = 16
 ITERS = 5
+
+
+def by_each_axis(value, one, other):
+    partial = lax.psum(value, one)
+    return lax.psum(partial, other)
 
 
 def padded_2(cells, sides, width):
@@ -111,13 +116,14 @@
         candidate = apply_operator(krylov_basis[j], inverse, coarse_links)
         local_pairs = [complex_dot(krylov_basis[i], candidate) for i in range(j + 1)]
         whole_local = complex_dot(candidate, candidate)[0]
-        proj_reals, proj_imags, whole_sq = lax.psum(
+        proj_reals, proj_imags, whole_sq = by_each_axis(
             (
                 jnp.stack([entry[0] for entry in local_pairs]),
                 jnp.stack([entry[1] for entry in local_pairs]),
                 whole_local,
             ),
-            ("ta", "gz", "xy"),
+            ("gz", "xy"),
+            "ta",
         )
         for i in range(j + 1):
             candidate = candidate - scaled(proj_reals[i], proj_imags[i], krylov_basis[i])

time: 573 us -> 544 us (0.949)
  blocking collectives: 240 us -> 223 us
  waiting for transfers between devices: 35.3 us -> 25.3 us
    ppermute x18, waiting for transfers between devices: 28.5 us -> 9.56 us  [padded_2(): lax.ppermute(tail, axis, [(i, (i + 1) % count) for i in range(count)])]
    psum x5 -> x10, blocking collectives: 198 us -> 181 us  [the longest x5 153 us: by_each_axis(): partial = lax.psum(value, one)]
    ppermute x18, waiting for transfers between devices: 6.81 us -> 15.7 us  [padded_2(): lax.ppermute(head, axis, [((i + 1) % count, i) for i in range(count)])]
    ppermute x18, starting transfers between devices: 26.5 us -> 18.5 us  [padded_2(): lax.ppermute(head, axis, [((i + 1) % count, i) for i in range(count)])]
    ppermute x18, starting transfers between devices: 5.81 us -> 13.1 us  [padded_2(): lax.ppermute(tail, axis, [(i, (i + 1) % count) for i in range(count)])]
  transfers between devices with their start and end apart: 36 -> 36, of which waited for: 16 -> 11; matrix products, arithmetic and copies ran while one was open for 12% -> 13% of each run, Pallas kernels for 0% -> 0%
where the time goes in v1:
time: 544 us; the launch traced here: 534 us
  blocking collectives  223 us (41%)
  other arithmetic  112 us (21%)
  between operations  88.9 us (16%)
  local copies, waits for them, and re-layouts  51.8 us (10%)
  starting transfers between devices  31.6 us (6%)
  waiting for transfers between devices  25.3 us (5%)
    psum x5, blocking collectives, by_each_axis(): partial = lax.psum(value, one)  153 us
    reduce_sum x24, other arithmetic, block_apply(): real_part = jnp.sum(real_blocks * vec_real - imag_blocks * vec_imag, axis=1)  65.3 us
    psum x1, blocking collectives, per_device(): norm_sq = lax.psum(complex_dot(source, source)[0], ('ta', 'gz', 'xy'))  42.2 us
    psum x5, blocking collectives, by_each_axis(): return lax.psum(partial, other)  27.8 us
    scatter x30, local copies, waits for them, and re-layouts, per_device(): hessenberg.at[0, i, j].set(proj_reals[i]).at[1, i, j].set(proj_imags[i])  25.8 us
    ppermute x18, starting transfers between devices, padded_2(): lax.ppermute(head, axis, [((i + 1) % count, i) for i in range(count)])  18.5 us
    ppermute x18, waiting for transfers between devices, padded_2(): lax.ppermute(head, axis, [((i + 1) % count, i) for i in range(count)])  15.7 us
    sub x15, other arithmetic, scaled(): coef_real * vector[0] - coef_imag * vector[1]  13.2 us
  transfers between devices with their start and end apart: 36, of which 11 were waited for; matrix products, arithmetic and copies ran while one was open for 13% of the time, Pallas kernels for 0%

profile of v1, /device:TPU:0, one launch (start us, length us, event | category | flops | bytes accessed | tf_op | source)
XLA Modules:
  0.0 533.6 jit_solution(13808259968086942491)
XLA Ops:
  2.1 42.2 %psum.217 = f32[]{:T(128)} all-reduce(f32[]{:T(128)} %add_reduce_fusion.20), channel_id=1, replica_groups=mesh['ta'=2,'gz'=4,'xy'=4] {'ta','gz','xy'}, use_global_device_ids=true, to_apply=%region_1.0 | all-reduce | flops 1 | bytes 8 | tf_op jit(solution)/shard_map/psum | solution.py:111
  53.1 3.7 fusion.169
  59.2 3.0 fusion.25
  63.5 4.9 collective-permute-done.3
  68.4 3.8 fusion.97
  73.8 31.4 %all-reduce.6 = (f32[1]{0:T(128)}, f32[1]{0:T(128)}, f32[]{:T(128)}) all-reduce(f32[1]{0:T(128)} %bitcast.81, f32[1]{0:T(128)} %bitcast.83, f32[]{:T(128)} %get-tuple-element.653), channel_id=1, replica_groups=mesh['ta'=2,'gz'=4,'xy'=4] {'gz','xy'}, use_global_device_ids=true, to_apply=%region_21.22 | all-reduce | flops 3 | bytes 24 | tf_op jit(solution)/shard_map/psum | solution.py:11
  105.1 5.5 %all-reduce.11 = (f32[1]{0:T(128)}, f32[1]{0:T(128)}, f32[]{:T(128)}) all-reduce(f32[1]{0:T(128)} %get-tuple-element.666, f32[1]{0:T(128)} %get-tuple-element.667, f32[]{:T(128)} %get-tuple-element.668), channel_id=1, replica_groups=mesh['ta'=2,'gz'=4,'xy'=4] {'ta'}, use_global_device_ids=true, to_apply=%region_22.23 | all-reduce | flops 3 | bytes 24 | tf_op jit(solution)/shard_map/psum | solution.py:12
  122.6 3.7 fusion.173
  126.5 3.8 collective-permute-start.8
  134.6 3.7 fusion.101
  142.7 31.9 %all-reduce.5 = (f32[2]{0:T(128)S(1)}, f32[2]{0:T(128)S(1)}, f32[]{:T(128)}) all-reduce(f32[2]{0:T(128)S(1)} %pad_maximum_fusion.30, f32[2]{0:T(128)S(1)} %pad_maximum_fusion.31, f32[]{:T(128)} %get-tuple-element.650), channel_id=1, replica_groups=mesh['ta'=2,'gz'=4,'xy'=4] {'gz','xy'}, use_global_device_ids=true, to_apply=%region_49.50 | all-reduce | flops 5 | bytes 40 | tf_op jit(solution)/shard_map/psum | solution.py:11
  174.6 5.5 %all-reduce.10 = (f32[2]{0:T(128)S(1)}, f32[2]{0:T(128)S(1)}, f32[]{:T(128)}) all-reduce(f32[2]{0:T(128)S(1)} %get-tuple-element.663, f32[2]{0:T(128)S(1)} %get-tuple-element.664, f32[]{:T(128)} %get-tuple-element.665), channel_id=1, replica_groups=mesh['ta'=2,'gz'=4,'xy'=4] {'ta'}, use_global_device_ids=true, to_apply=%region_50.51 | all-reduce | flops 5 | bytes 40 | tf_op jit(solution)/shard_map/psum | solution.py:12
  193.9 3.7 fusion.177
  203.2 3.9 collective-permute-done.14
  207.2 3.7 fusion.105
  216.5 30.0 %all-reduce.4 = (f32[3]{0:T(128)S(1)}, f32[3]{0:T(128)S(1)}, f32[]{:T(128)}) all-reduce(f32[3]{0:T(128)S(1)} %pad_maximum_fusion.32, f32[3]{0:T(128)S(1)} %pad_maximum_fusion.33, f32[]{:T(128)} %get-tuple-element.647), channel_id=1, replica_groups=mesh['ta'=2,'gz'=4,'xy'=4] {'gz','xy'}, use_global_device_ids=true, to_apply=%region_80.81 | all-reduce | flops 7 | bytes 56 | tf_op jit(solution)/shard_map/psum | solution.py:11
  246.4 5.5 %all-reduce.9 = (f32[3]{0:T(128)S(1)}, f32[3]{0:T(128)S(1)}, f32[]{:T(128)}) all-reduce(f32[3]{0:T(128)S(1)} %get-tuple-element.660, f32[3]{0:T(128)S(1)} %get-tuple-element.661, f32[]{:T(128)} %get-tuple-element.662), channel_id=1, replica_groups=mesh['ta'=2,'gz'=4,'xy'=4] {'ta'}, use_global_device_ids=true, to_apply=%region_81.82 | all-reduce | flops 7 | bytes 56 | tf_op jit(solution)/shard_map/psum | solution.py:12
  270.5 3.7 fusion.181
  279.6 3.8 collective-permute-done.20
  283.4 3.7 fusion.109
  294.2 30.1 %all-reduce.3 = (f32[4]{0:T(128)S(1)}, f32[4]{0:T(128)S(1)}, f32[]{:T(128)}) all-reduce(f32[4]{0:T(128)S(1)} %pad_maximum_fusion.34, f32[4]{0:T(128)S(1)} %pad_maximum_fusion.35, f32[]{:T(128)} %get-tuple-element.642), channel_id=1, replica_groups=mesh['ta'=2,'gz'=4,'xy'=4] {'gz','xy'}, use_global_device_ids=true, to_apply=%region_113.114 | all-reduce | flops 9 | bytes 72 | tf_op jit(solution)/shard_map/psum | solution.py:11
  324.3 5.6 %all-reduce.8 = (f32[4]{0:T(128)S(1)}, f32[4]{0:T(128)S(1)}, f32[]{:T(128)}) all-reduce(f32[4]{0:T(128)S(1)} %get-tuple-element.657, f32[4]{0:T(128)S(1)} %get-tuple-element.658, f32[]{:T(128)} %get-tuple-element.659), channel_id=1, replica_groups=mesh['ta'=2,'gz'=4,'xy'=4] {'ta'}, use_global_device_ids=true, to_apply=%region_114.115 | all-reduce | flops 9 | bytes 72 | tf_op jit(solution)/shard_map/psum | solution.py:12
  349.5 3.7 fusion.185
  355.7 3.0 fusion.41
  358.6 3.7 collective-permute-done.26
  362.4 3.7 fusion.113
  368.4 3.2 stack.868
  371.6 3.3 stack.862
  374.9 30.0 %all-reduce.2 = (f32[5]{0:T(128)S(1)}, f32[5]{0:T(128)S(1)}, f32[]{:T(128)}) all-reduce(f32[5]{0:T(128)S(1)} %stack.862, f32[5]{0:T(128)S(1)} %stack.868, f32[]{:T(128)} %get-tuple-element.766), channel_id=1, replica_groups=mesh['ta'=2,'gz'=4,'xy'=4] {'gz','xy'}, use_global_device_ids=true, to_apply=%region_148.149 | all-reduce | flops 11 | bytes 88 | tf_op jit(solution)/shard_map/psum | solution.py:11
  404.8 5.5 %all-reduce.7 = (f32[5]{0:T(128)S(1)}, f32[5]{0:T(128)S(1)}, f32[]{:T(128)}) all-reduce(f32[5]{0:T(128)S(1)} %get-tuple-element.654, f32[5]{0:T(128)S(1)} %get-tuple-element.655, f32[]{:T(128)} %get-tuple-element.656), channel_id=1, replica_groups=mesh['ta'=2,'gz'=4,'xy'=4] {'ta'}, use_global_device_ids=true, to_apply=%region_149.150 | all-reduce | flops 11 | bytes 88 | tf_op jit(solution)/shard_map/psum | solution.py:12
  516.4 3.7 fusion.189
  528.1 3.7 fusion.117
  (295 shorter events, 144.8 us)
Async XLA Ops:
  45.7 11.1 %collective-permute-start = (f32[2,48,1,1,128]{4,3,2,1,0:T(1,128)S(1)}, f32[2,48,1,1,128]{4,3,2,1,0:T(1,128)S(1)}, u32[]{:S(2)}, u32[]{:S(2)}) collective-permute-start(f32[2,48,1,1,128]{4,3,2,1,0:T(1,128)S(1)} %broadcast_divide_fusion), channel_id=1, source_target_pairs={{16,0},{0,16},{17,1},{1,17},{18,2},{2,18},{19,3},{3,19},{20,4},{4,... | collective-permute-start | bytes 147464 | tf_op jit(solution)/shard_map/ppermute | solution.py:24
  48.1 8.7 %collective-permute-start.1 = (f32[2,48,1,1,128]{4,3,2,1,0:T(1,128)S(1)}, f32[2,48,1,1,128]{4,3,2,1,0:T(1,128)S(1)}, u32[]{:S(2)}, u32[]{:S(2)}) collective-permute-start(f32[2,48,1,1,128]{4,3,2,1,0:T(1,128)S(1)} %broadcast_divide_fusion), channel_id=1, source_target_pairs={{0,16},{16,0},{1,17},{17,1},{2,18},{18,2},{3,19},{19,3},{4,20},{20... | collective-permute-start | bytes 147464 | tf_op jit(solution)/shard_map/ppermute | solution.py:22
  48.3 3.9 collective-permute-start.4
  48.4 4.4 collective-permute-start.5
  57.0 6.5 %collective-permute-start.2 = (f32[2,48,3,1,128]{4,3,2,1,0:T(1,128)S(1)}, f32[2,48,3,1,128]{4,3,2,1,0:T(1,128)S(1)}, u32[]{:S(2)}, u32[]{:S(2)}) collective-permute-start(f32[2,48,3,1,128]{4,3,2,1,0:T(1,128)S(1)} %pad_maximum_fusion), channel_id=1, source_target_pairs={{4,0},{8,4},{12,8},{0,12},{5,1},{9,5},{13,9},{1,13},{6,2},{10,6},{... | collective-permute-start | bytes 442376 | tf_op jit(solution)/shard_map/ppermute | solution.py:24
  59.2 9.1 %collective-permute-start.3 = (f32[2,48,3,1,128]{4,3,2,1,0:T(1,128)S(1)}, f32[2,48,3,1,128]{4,3,2,1,0:T(1,128)S(1)}, u32[]{:S(2)}, u32[]{:S(2)}) collective-permute-start(f32[2,48,3,1,128]{4,3,2,1,0:T(1,128)S(1)} %pad_maximum_fusion), channel_id=1, source_target_pairs={{0,4},{4,8},{8,12},{12,0},{1,5},{5,9},{9,13},{13,1},{2,6},{6,10},{... | collective-permute-start | bytes 442376 | tf_op jit(solution)/shard_map/ppermute | solution.py:22
  116.2 10.1 %collective-permute-start.6 = (f32[2,48,1,1,128]{4,3,2,1,0:T(1,128)S(1)}, f32[2,48,1,1,128]{4,3,2,1,0:T(1,128)S(1)}, u32[]{:S(2)}, u32[]{:S(2)}) collective-permute-start(f32[2,48,1,1,128]{4,3,2,1,0:T(1,128)S(1)} %fusion.222), channel_id=1, source_target_pairs={{16,0},{0,16},{17,1},{1,17},{18,2},{2,18},{19,3},{3,19},{20,4},{4,... | collective-permute-start | bytes 147464 | tf_op jit(solution)/shard_map/ppermute | solution.py:24
  118.0 8.3 %collective-permute-start.7 = (f32[2,48,1,1,128]{4,3,2,1,0:T(1,128)S(1)}, f32[2,48,1,1,128]{4,3,2,1,0:T(1,128)S(1)}, u32[]{:S(2)}, u32[]{:S(2)}) collective-permute-start(f32[2,48,1,1,128]{4,3,2,1,0:T(1,128)S(1)} %fusion.222), channel_id=1, source_target_pairs={{0,16},{16,0},{1,17},{17,1},{2,18},{18,2},{3,19},{19,3},{4,20},{20... | collective-permute-start | bytes 147464 | tf_op jit(solution)/shard_map/ppermute | solution.py:22
  126.4 8.1 %collective-permute-start.9 = (f32[2,48,3,1,128]{4,3,2,1,0:T(1,128)S(1)}, f32[2,48,3,1,128]{4,3,2,1,0:T(1,128)S(1)}, u32[]{:S(2)}, u32[]{:S(2)}) collective-permute-start(f32[2,48,3,1,128]{4,3,2,1,0:T(1,128)S(1)} %pad_maximum_fusion.1), channel_id=1, source_target_pairs={{0,4},{4,8},{8,12},{12,0},{1,5},{5,9},{9,13},{13,1},{2,6},{6,10},{... | collective-permute-start | bytes 442376 | tf_op jit(solution)/shard_map/ppermute | solution.py:22
  126.5 8.1 %collective-permute-start.8 = (f32[2,48,3,1,128]{4,3,2,1,0:T(1,128)S(1)}, f32[2,48,3,1,128]{4,3,2,1,0:T(1,128)S(1)}, u32[]{:S(2)}, u32[]{:S(2)}) collective-permute-start(f32[2,48,3,1,128]{4,3,2,1,0:T(1,128)S(1)} %pad_maximum_fusion.1), channel_id=1, source_target_pairs={{4,0},{8,4},{12,8},{0,12},{5,1},{9,5},{13,9},{1,13},{6,2},{10,6},{... | collective-permute-start | bytes 442376 | tf_op jit(solution)/shard_map/ppermute | solution.py:24
  187.0 10.6 %collective-permute-start.12 = (f32[2,48,1,1,128]{4,3,2,1,0:T(1,128)S(1)}, f32[2,48,1,1,128]{4,3,2,1,0:T(1,128)S(1)}, u32[]{:S(2)}, u32[]{:S(2)}) collective-permute-start(f32[2,48,1,1,128]{4,3,2,1,0:T(1,128)S(1)} %fusion.262), channel_id=1, source_target_pairs={{16,0},{0,16},{17,1},{1,17},{18,2},{2,18},{19,3},{3,19},{20,4},{4,... | collective-permute-start | bytes 147464 | tf_op jit(solution)/shard_map/ppermute | solution.py:24
  188.8 8.7 %collective-permute-start.13 = (f32[2,48,1,1,128]{4,3,2,1,0:T(1,128)S(1)}, f32[2,48,1,1,128]{4,3,2,1,0:T(1,128)S(1)}, u32[]{:S(2)}, u32[]{:S(2)}) collective-permute-start(f32[2,48,1,1,128]{4,3,2,1,0:T(1,128)S(1)} %fusion.262), channel_id=1, source_target_pairs={{0,16},{16,0},{1,17},{17,1},{2,18},{18,2},{3,19},{19,3},{4,20},{20... | collective-permute-start | bytes 147464 | tf_op jit(solution)/shard_map/ppermute | solution.py:22
  189.4 4.1 collective-permute-start.16
  189.4 4.0 collective-permute-start.17
  197.7 9.4 %collective-permute-start.14 = (f32[2,48,3,1,128]{4,3,2,1,0:T(1,128)S(1)}, f32[2,48,3,1,128]{4,3,2,1,0:T(1,128)S(1)}, u32[]{:S(2)}, u32[]{:S(2)}) collective-permute-start(f32[2,48,3,1,128]{4,3,2,1,0:T(1,128)S(1)} %pad_maximum_fusion.2), channel_id=1, source_target_pairs={{4,0},{8,4},{12,8},{0,12},{5,1},{9,5},{13,9},{1,13},{6,2},{10,6},{... | collective-permute-start | bytes 442376 | tf_op jit(solution)/shard_map/ppermute | solution.py:24
  198.2 8.9 %collective-permute-start.15 = (f32[2,48,3,1,128]{4,3,2,1,0:T(1,128)S(1)}, f32[2,48,3,1,128]{4,3,2,1,0:T(1,128)S(1)}, u32[]{:S(2)}, u32[]{:S(2)}) collective-permute-start(f32[2,48,3,1,128]{4,3,2,1,0:T(1,128)S(1)} %pad_maximum_fusion.2), channel_id=1, source_target_pairs={{0,4},{4,8},{8,12},{12,0},{1,5},{5,9},{9,13},{13,1},{2,6},{6,10},{... | collective-permute-start | bytes 442376 | tf_op jit(solution)/shard_map/ppermute | solution.py:22
  260.2 13.9 %collective-permute-start.18 = (f32[2,48,1,1,128]{4,3,2,1,0:T(1,128)S(1)}, f32[2,48,1,1,128]{4,3,2,1,0:T(1,128)S(1)}, u32[]{:S(2)}, u32[]{:S(2)}) collective-permute-start(f32[2,48,1,1,128]{4,3,2,1,0:T(1,128)S(1)} %fusion.263), channel_id=1, source_target_pairs={{16,0},{0,16},{17,1},{1,17},{18,2},{2,18},{19,3},{3,19},{20,4},{4,... | collective-permute-start | bytes 147464 | tf_op jit(solution)/shard_map/ppermute | solution.py:24
  262.1 12.1 %collective-permute-start.19 = (f32[2,48,1,1,128]{4,3,2,1,0:T(1,128)S(1)}, f32[2,48,1,1,128]{4,3,2,1,0:T(1,128)S(1)}, u32[]{:S(2)}, u32[]{:S(2)}) collective-permute-start(f32[2,48,1,1,128]{4,3,2,1,0:T(1,128)S(1)} %fusion.263), channel_id=1, source_target_pairs={{0,16},{16,0},{1,17},{17,1},{2,18},{18,2},{3,19},{19,3},{4,20},{20... | collective-permute-start | bytes 147464 | tf_op jit(solution)/shard_map/ppermute | solution.py:22
  262.6 7.5 %collective-permute-start.22 = (f32[2,48,1,1,16]{4,3,2,1,0:T(1,128)S(1)}, f32[2,48,1,1,16]{4,3,2,1,0:T(1,128)S(1)}, u32[]{:S(2)}, u32[]{:S(2)}) collective-permute-start(f32[2,48,1,1,16]{4,3,2,1,0:T(1,128)S(1)} %get-tuple-element.812), channel_id=1, source_target_pairs={{1,0},{2,1},{3,2},{0,3},{5,4},{6,5},{7,6},{4,7},{9,8},{10,9},{11,1... | collective-permute-start | bytes 18440 | tf_op jit(solution)/shard_map/ppermute | solution.py:24
  262.7 7.4 %collective-permute-start.23 = (f32[2,48,1,1,16]{4,3,2,1,0:T(1,128)S(1)}, f32[2,48,1,1,16]{4,3,2,1,0:T(1,128)S(1)}, u32[]{:S(2)}, u32[]{:S(2)}) collective-permute-start(f32[2,48,1,1,16]{4,3,2,1,0:T(1,128)S(1)} %get-tuple-element.811), channel_id=1, source_target_pairs={{0,1},{1,2},{2,3},{3,0},{4,5},{5,6},{6,7},{7,4},{8,9},{9,10},{10,1... | collective-permute-start | bytes 18440 | tf_op jit(solution)/shard_map/ppermute | solution.py:22
  274.3 9.0 %collective-permute-start.20 = (f32[2,48,3,1,128]{4,3,2,1,0:T(1,128)S(1)}, f32[2,48,3,1,128]{4,3,2,1,0:T(1,128)S(1)}, u32[]{:S(2)}, u32[]{:S(2)}) collective-permute-start(f32[2,48,3,1,128]{4,3,2,1,0:T(1,128)S(1)} %pad_maximum_fusion.3), channel_id=1, source_target_pairs={{4,0},{8,4},{12,8},{0,12},{5,1},{9,5},{13,9},{1,13},{6,2},{10,6},{... | collective-permute-start | bytes 442376 | tf_op jit(solution)/shard_map/ppermute | solution.py:24
  274.4 8.9 %collective-permute-start.21 = (f32[2,48,3,1,128]{4,3,2,1,0:T(1,128)S(1)}, f32[2,48,3,1,128]{4,3,2,1,0:T(1,128)S(1)}, u32[]{:S(2)}, u32[]{:S(2)}) collective-permute-start(f32[2,48,3,1,128]{4,3,2,1,0:T(1,128)S(1)} %pad_maximum_fusion.3), channel_id=1, source_target_pairs={{0,4},{4,8},{8,12},{12,0},{1,5},{5,9},{9,13},{13,1},{2,6},{6,10},{... | collective-permute-start | bytes 442376 | tf_op jit(solution)/shard_map/ppermute | solution.py:22
  339.6 13.6 %collective-permute-start.24 = (f32[2,48,1,1,128]{4,3,2,1,0:T(1,128)S(1)}, f32[2,48,1,1,128]{4,3,2,1,0:T(1,128)S(1)}, u32[]{:S(2)}, u32[]{:S(2)}) collective-permute-start(f32[2,48,1,1,128]{4,3,2,1,0:T(1,128)S(1)} %fusion.246), channel_id=1, source_target_pairs={{16,0},{0,16},{17,1},{1,17},{18,2},{2,18},{19,3},{3,19},{20,4},{4,... | collective-permute-start | bytes 147464 | tf_op jit(solution)/shard_map/ppermute | solution.py:24
  341.4 11.8 %collective-permute-start.25 = (f32[2,48,1,1,128]{4,3,2,1,0:T(1,128)S(1)}, f32[2,48,1,1,128]{4,3,2,1,0:T(1,128)S(1)}, u32[]{:S(2)}, u32[]{:S(2)}) collective-permute-start(f32[2,48,1,1,128]{4,3,2,1,0:T(1,128)S(1)} %fusion.246), channel_id=1, source_target_pairs={{0,16},{16,0},{1,17},{17,1},{2,18},{18,2},{3,19},{19,3},{4,20},{20... | collective-permute-start | bytes 147464 | tf_op jit(solution)/shard_map/ppermute | solution.py:22
  342.0 7.2 %collective-permute-start.28 = (f32[2,48,1,1,16]{4,3,2,1,0:T(1,128)S(1)}, f32[2,48,1,1,16]{4,3,2,1,0:T(1,128)S(1)}, u32[]{:S(2)}, u32[]{:S(2)}) collective-permute-start(f32[2,48,1,1,16]{4,3,2,1,0:T(1,128)S(1)} %get-tuple-element.778), channel_id=1, source_target_pairs={{1,0},{2,1},{3,2},{0,3},{5,4},{6,5},{7,6},{4,7},{9,8},{10,9},{11,1... | collective-permute-start | bytes 18440 | tf_op jit(solution)/shard_map/ppermute | solution.py:24
  342.0 7.1 %collective-permute-start.29 = (f32[2,48,1,1,16]{4,3,2,1,0:T(1,128)S(1)}, f32[2,48,1,1,16]{4,3,2,1,0:T(1,128)S(1)}, u32[]{:S(2)}, u32[]{:S(2)}) collective-permute-start(f32[2,48,1,1,16]{4,3,2,1,0:T(1,128)S(1)} %get-tuple-element.777), channel_id=1, source_target_pairs={{0,1},{1,2},{2,3},{3,0},{4,5},{5,6},{6,7},{7,4},{8,9},{9,10},{10,1... | collective-permute-start | bytes 18440 | tf_op jit(solution)/shard_map/ppermute | solution.py:22
  353.4 9.0 %collective-permute-start.26 = (f32[2,48,3,1,128]{4,3,2,1,0:T(1,128)S(1)}, f32[2,48,3,1,128]{4,3,2,1,0:T(1,128)S(1)}, u32[]{:S(2)}, u32[]{:S(2)}) collective-permute-start(f32[2,48,3,1,128]{4,3,2,1,0:T(1,128)S(1)} %pad_maximum_fusion.4), channel_id=1, source_target_pairs={{4,0},{8,4},{12,8},{0,12},{5,1},{9,5},{13,9},{1,13},{6,2},{10,6},{... | collective-permute-start | bytes 442376 | tf_op jit(solution)/shard_map/ppermute | solution.py:24
  353.5 8.9 %collective-permute-start.27 = (f32[2,48,3,1,128]{4,3,2,1,0:T(1,128)S(1)}, f32[2,48,3,1,128]{4,3,2,1,0:T(1,128)S(1)}, u32[]{:S(2)}, u32[]{:S(2)}) collective-permute-start(f32[2,48,3,1,128]{4,3,2,1,0:T(1,128)S(1)} %pad_maximum_fusion.4), channel_id=1, source_target_pairs={{0,4},{4,8},{8,12},{12,0},{1,5},{5,9},{9,13},{13,1},{2,6},{6,10},{... | collective-permute-start | bytes 442376 | tf_op jit(solution)/shard_map/ppermute | solution.py:22
  509.8 10.3 %collective-permute-start.30 = (f32[2,48,1,1,128]{4,3,2,1,0:T(1,128)S(1)}, f32[2,48,1,1,128]{4,3,2,1,0:T(1,128)S(1)}, u32[]{:S(2)}, u32[]{:S(2)}) collective-permute-start(f32[2,48,1,1,128]{4,3,2,1,0:T(1,128)S(1)} %maximum_add_fusion.11), channel_id=1, source_target_pairs={{16,0},{0,16},{17,1},{1,17},{18,2},{2,18},{19,3},{3,19},{20,4},{4,... | collective-permute-start | bytes 147464 | tf_op jit(solution)/shard_map/ppermute | solution.py:24
  511.6 8.5 %collective-permute-start.31 = (f32[2,48,1,1,128]{4,3,2,1,0:T(1,128)S(1)}, f32[2,48,1,1,128]{4,3,2,1,0:T(1,128)S(1)}, u32[]{:S(2)}, u32[]{:S(2)}) collective-permute-start(f32[2,48,1,1,128]{4,3,2,1,0:T(1,128)S(1)} %maximum_add_fusion.11), channel_id=1, source_target_pairs={{0,16},{16,0},{1,17},{17,1},{2,18},{18,2},{3,19},{19,3},{4,20},{20... | collective-permute-start | bytes 147464 | tf_op jit(solution)/shard_map/ppermute | solution.py:22
  520.2 7.7 %collective-permute-start.32 = (f32[2,48,3,1,128]{4,3,2,1,0:T(1,128)S(1)}, f32[2,48,3,1,128]{4,3,2,1,0:T(1,128)S(1)}, u32[]{:S(2)}, u32[]{:S(2)}) collective-permute-start(f32[2,48,3,1,128]{4,3,2,1,0:T(1,128)S(1)} %pad_maximum_fusion.5), channel_id=1, source_target_pairs={{4,0},{8,4},{12,8},{0,12},{5,1},{9,5},{13,9},{1,13},{6,2},{10,6},{... | collective-permute-start | bytes 442376 | tf_op jit(solution)/shard_map/ppermute | solution.py:24
  520.3 7.7 %collective-permute-start.33 = (f32[2,48,3,1,128]{4,3,2,1,0:T(1,128)S(1)}, f32[2,48,3,1,128]{4,3,2,1,0:T(1,128)S(1)}, u32[]{:S(2)}, u32[]{:S(2)}) collective-permute-start(f32[2,48,3,1,128]{4,3,2,1,0:T(1,128)S(1)} %pad_maximum_fusion.5), channel_id=1, source_target_pairs={{0,4},{4,8},{8,12},{12,0},{1,5},{5,9},{9,13},{13,1},{2,6},{6,10},{... | collective-permute-start | bytes 442376 | tf_op jit(solution)/shard_map/ppermute | solution.py:22
  (8 other events, 78.8 us)
